TPU v7x, 32 devices: a whole 2x2x4 slice. The times are simulated.
32 devices in a mesh: tp: 8 (over z, y), rep: 4 (over x, core).
Axes of the slice: x: 2, y: 2, z: 4, core: 2. Of those that a mesh axis runs over, the one named last changes fastest.
Arguments:
- tokens: bfloat16 [1536, 8192], P('rep', 'tp'), may hold values from -6 to 6
- row_lengths: int32 [8], P('rep'), may hold values from 1 to 192
- attn_gain: float32 [8192], P('tp'), may hold values from 0.1 to 1.9
- query_weight: bfloat16 [8192, 4096], P('rep', 'tp'), may hold values from -2 to 2
- key_weight: bfloat16 [8192, 512], P('rep', 'tp'), may hold values from -2 to 2
- value_matrix: bfloat16 [8192, 512], P('rep', 'tp'), may hold values from -0.0625 to 0.0625
- output_weight: bfloat16 [4096, 8192], P('rep', 'tp'), may hold values from -0.09375 to 0.09375
- final_gain: float32 [8192], P('tp'), may hold values from 0.1 to 1.9
- value_head: float32 [8192, 6], P('tp'), may hold values from -0.0625 to 0.0625
Outputs:
- resid_out: bfloat16 [1536, 8192], P('rep', 'tp')
- objective_scores: float32 [1536, 6], P('rep')
All inputs are finite; a program needn't handle non-finite values.
Results may differ from a plain program's by a relative error of at most 0.025.
Values may be sent and summed in bfloat16 or wider, within the bound.
A program may use at most 64 MiB of HBM per device.

v0:
```python
import jax
import jax.numpy as jnp
from jax import lax
from jax.sharding import PartitionSpec as P

KEY_VALUE_HEADS = 4
HEAD_SIZE = 128


EPS = 1e-05


def local(
    tokens,
    row_lengths,
    attn_gain,
    query_weight,
    key_weight,
    value_matrix,
    output_weight,
    final_gain,
    value_head,
):
    width = tokens.shape[1] * lax.axis_size("tp")
    xfloat = tokens.astype(jnp.float32)
    total = lax.psum(jnp.sum(xfloat * xfloat, axis=1), "tp")
    first_scale = lax.rsqrt(total / width + EPS)[:, None]
    normed = lax.all_gather(
        (xfloat * first_scale * attn_gain).astype(jnp.bfloat16), "tp", axis=1, tiled=True
    )
    rows_here = normed.shape[0]
    head_cols = query_weight.shape[1]
    pieces = (
        lax.all_gather(query_weight, "rep", axis=0, tiled=True),
        lax.all_gather(key_weight, "rep", axis=0, tiled=True),
        lax.all_gather(value_matrix, "rep", axis=0, tiled=True),
    )
    columns = normed
    query, key_rows, value_rows = tuple(
        (jnp.dot(columns, piece, preferred_element_type=jnp.float32) for piece in pieces)
    )
    query = query.astype(jnp.bfloat16)
    key_rows = key_rows.astype(jnp.bfloat16)
    value_rows = value_rows.astype(jnp.bfloat16)
    key_full, value_full = (
        lax.all_gather(key_rows, "tp", axis=1, tiled=True),
        lax.all_gather(value_rows, "tp", axis=1, tiled=True),
    )
    local_heads = head_cols // HEAD_SIZE
    sequence_rows = row_lengths.shape[0]
    row_length_count = rows_here // sequence_rows
    first_head = lax.axis_index("tp") * local_heads
    key_value_index = (first_head + jnp.arange(local_heads, dtype=jnp.int32)) % KEY_VALUE_HEADS
    query4 = query.reshape(sequence_rows, row_length_count, local_heads, HEAD_SIZE)
    key_tensor4 = jnp.take(
        key_full.reshape(sequence_rows, row_length_count, KEY_VALUE_HEADS, HEAD_SIZE),
        key_value_index,
        axis=2,
    )
    value_tensor4 = jnp.take(
        value_full.reshape(sequence_rows, row_length_count, KEY_VALUE_HEADS, HEAD_SIZE),
        key_value_index,
        axis=2,
    )
    scores = jnp.einsum(
        "rqhd,rkhd->rhqk", query4, key_tensor4, preferred_element_type=jnp.float32
    ) * (1.0 / HEAD_SIZE**0.5)
    position = jnp.arange(row_length_count, dtype=jnp.int32)
    causal = position[None, :] <= position[:, None]
    allowed = causal[None, None, :, :] & (
        position[None, None, None, :] < row_lengths[:, None, None, None]
    )
    scores = jnp.where(allowed, scores, jnp.float32(-1e30))
    scores = scores - jnp.max(scores, axis=3, keepdims=True)
    expo = jnp.exp(scores)
    probs = (expo / jnp.sum(expo, axis=3, keepdims=True)).astype(jnp.bfloat16)
    attended = jnp.einsum(
        "rhqk,rkhd->rqhd", probs, value_tensor4, preferred_element_type=jnp.float32
    )
    attended = attended.astype(jnp.bfloat16).reshape(rows_here, head_cols)
    mixed_all = lax.all_gather(attended, "tp", axis=1, tiled=True)
    columns = mixed_all
    update = jnp.dot(
        columns,
        lax.all_gather(output_weight, "rep", axis=0, tiled=True),
        preferred_element_type=jnp.float32,
    )
    resid_out = (xfloat + update).astype(jnp.bfloat16)
    rfloat = resid_out.astype(jnp.float32)
    squares = jnp.sum(rfloat * rfloat, axis=1)
    local_scores = jnp.dot(rfloat * final_gain, value_head, precision=lax.Precision.HIGHEST)
    total_out, weighted = lax.psum((squares, local_scores), "tp")
    logits = weighted * lax.rsqrt(total_out / width + EPS)[:, None]
    live = (position[None, :] < row_lengths[:, None]).reshape(rows_here, 1)
    objective_scores = jnp.where(live, logits, jnp.float32(0.0))
    return (resid_out, objective_scores)


def solution(mesh):
    in_specs = (
        P("rep", "tp"),
        P("rep"),
        P("tp"),
        P("rep", "tp"),
        P("rep", "tp"),
        P("rep", "tp"),
        P("rep", "tp"),
        P("tp"),
        P("tp", None),
    )
    out_specs = (P("rep", "tp"), P("rep", None))
    return jax.shard_map(local, mesh=mesh, in_specs=in_specs, out_specs=out_specs, check_vma=False)
```

profile of v0, /device:TPU:0, one launch (start us, length us, event | category | flops | bytes accessed | tf_op | source)
XLA Modules:
  0.0 382.7 jit_solution(16926781889026036177)
XLA Ops:
  7.2 0.7 all-gather.9.cloned.1.call-update
  8.0 1.4 fusion.4
  9.3 23.1 %psum.21 = f32[384]{0:T(512)S(1)} all-reduce(f32[384]{0:T(512)S(1)} %fusion.4), channel_id=1, replica_groups=mesh['tp'=8,'rep'=4] {'tp'}, use_global_device_ids=true, to_apply=%region_1.0 | all-reduce | flops 384 | bytes 3072 | tf_op jit(solution)/shard_map/psum | solution.py:26
  32.5 1.8 fusion.6
  34.4 0.7 all-gather.13.cloned.1.call-update
  35.1 0.5 all-gather.11.cloned.1.call-update
  35.7 0.5 all-gather.17.cloned.1.call-update
  36.5 0.1 broadcast_and_fusion
  36.6 93.9 %all-gather.7.cloned.1.call-done = bf16[384,8192]{1,0:T(8,128)(2,1)} async-done(((bf16[384,1024]{1,0:T(8,128)(2,1)}), bf16[384,8192]{1,0:T(8,128)(2,1)}) %all-gather.7.cloned.1.call-update) | async-done | bytes 6291472 | tf_op jit(solution)/shard_map/all_gather | solution.py:28
  130.5 5.1 %convolution_convert_fusion.3 = bf16[384,64]{0,1:T(8,128)(2,1)S(1)} fusion(bf16[384,8192]{1,0:T(8,128)(2,1)} %all-gather.7.cloned.1.call-done, bf16[8192,64]{0,1:T(8,128)(2,1)} %all-gather.9.cloned.1.call-done), kind=kOutput, calls=%fused_computation.22 | convolution fusion | flops 402677760 | bytes 7389184 | tf_op jit(solution)/shard_map/dot_general | solution.py:40
  135.6 31.0 %all_gather.26 = bf16[384,512]{0,1:T(8,128)(2,1)S(1)} all-gather(bf16[384,64]{0,1:T(8,128)(2,1)S(1)} %convolution_convert_fusion.3), channel_id=1, replica_groups=mesh['tp'=8,'rep'=4] {'tp'}, dimensions={1}, use_global_device_ids=true | all-gather | bytes 442368 | tf_op jit(solution)/shard_map/all_gather | solution.py:47
  166.6 0.3 reshape.108
  166.8 0.4 copy.14
  167.3 5.1 %convolution_convert_fusion.2 = bf16[384,64]{0,1:T(8,128)(2,1)S(1)} fusion(bf16[384,8192]{1,0:T(8,128)(2,1)} %all-gather.7.cloned.1.call-done, bf16[8192,64]{0,1:T(8,128)(2,1)} %all-gather.13.cloned.1.call-done), kind=kOutput, calls=%fused_computation.21 | convolution fusion | flops 402677760 | bytes 7389184 | tf_op jit(solution)/shard_map/dot_general | solution.py:40
  172.4 31.1 %all_gather.29 = bf16[384,512]{0,1:T(8,128)(2,1)S(1)} all-gather(bf16[384,64]{0,1:T(8,128)(2,1)S(1)} %convolution_convert_fusion.2), channel_id=1, replica_groups=mesh['tp'=8,'rep'=4] {'tp'}, dimensions={1}, use_global_device_ids=true | all-gather | bytes 442368 | tf_op jit(solution)/shard_map/all_gather | solution.py:46
  203.6 0.3 reshape.109
  203.8 0.4 copy.16
  204.3 0.6 gather_fusion
  204.9 0.6 gather_fusion.1
  205.6 0.1 select_bitcast_fusion.1
  205.7 1.0 all-gather.11.cloned.1.call-done
  206.7 8.6 %convolution_convert_fusion.1 = bf16[384,512]{1,0:T(8,128)(2,1)S(1)} fusion(bf16[384,8192]{1,0:T(8,128)(2,1)} %all-gather.7.cloned.1.call-done, bf16[8192,512]{1,0:T(8,128)(2,1)} %all-gather.11.cloned.1.call-done), kind=kOutput, calls=%fused_computation.19 | convolution fusion | flops 3221422080 | bytes 15073280 | tf_op jit(solution)/shard_map/dot_general | solution.py:40
  215.4 1.9 fusion.26
  217.3 2.0 fusion.9
  219.3 0.3 copy.21
  219.6 0.8 copy.47
  220.5 45.9 %all-gather.17.cloned.1.call-done = bf16[4096,1024]{1,0:T(8,128)(2,1)} async-done(((bf16[1024,1024]{1,0:T(8,128)(2,1)}), bf16[4096,1024]{1,0:T(8,128)(2,1)}) %all-gather.17.cloned.1.call-update) | async-done | bytes 8388624 | tf_op jit(solution)/shard_map/all_gather | solution.py:85
  266.4 65.2 %all-gather.15.cloned.1.call-done = bf16[384,4096]{1,0:T(8,128)(2,1)} async-done(((bf16[384,512]{1,0:T(8,128)(2,1)}), bf16[384,4096]{1,0:T(8,128)(2,1)}) %all-gather.15.cloned.1.call-update) | async-done | bytes 3145744 | tf_op jit(solution)/shard_map/all_gather | solution.py:81
  331.6 7.9 %fusion.3 = (f32[384]{0:T(512)S(1)}, bf16[384,1024]{1,0:T(8,128)(2,1)S(1)}) fusion(bf16[384,4096]{1,0:T(8,128)(2,1)} %all-gather.15.cloned.1.call-done, bf16[4096,1024]{1,0:T(8,128)(2,1)} %all-gather.17.cloned.1.call-done, bf16[384,1024]{1,0:T(8,128)(2,1)S(1)} %copy-done.1), kind=kOutput, calls=%fused_computation.10 | convolution fusion | flops 3223584256 | bytes 13108736 | tf_op jit(solution)/shard_map/dot_general | solution.py:83
  339.4 1.5 fusion.2
  340.9 34.3 %all-reduce = (f32[384,6]{0,1:T(8,128)S(1)}, f32[384]{0:T(512)S(1)}) all-reduce(f32[384,6]{0,1:T(8,128)S(1)} %fusion.2, f32[384]{0:T(512)S(1)} %get-tuple-element.9), channel_id=1, replica_groups=mesh['tp'=8,'rep'=4] {'tp'}, use_global_device_ids=true, to_apply=%region_4.6 | all-reduce | flops 2688 | bytes 21504 | tf_op jit(solution)/shard_map/psum | solution.py:92
  375.2 0.6 multiply_select_fusion.1
  (29 shorter events, 0.7 us)
Async XLA Ops:
  7.2 332.3 %copy-start = (f32[1024,6]{0,1:T(8,128)S(1)}, f32[1024,6]{0,1:T(8,128)}, u32[]{:S(2)}) copy-start(f32[1024,6]{0,1:T(8,128)} %param.19) | copy-start | bytes 73732
  7.2 25.3 %copy-start.1 = (bf16[384,1024]{1,0:T(8,128)(2,1)S(1)}, bf16[384,1024]{1,0:T(8,128)(2,1)}, u32[]{:S(2)}) copy-start(bf16[384,1024]{1,0:T(8,128)(2,1)} %param.11) | copy-start | bytes 2359300
  7.2 29.4 %all-gather.9.cloned.1.call-start = ((), (), s32[]{:S(2)}) async-start(), calls=%async_computation.1 | async-start | bytes 1310720 | tf_op jit(solution)/shard_map/all_gather | solution.py:36
  7.9 122.6 %all-gather.7.cloned.1.call-start = ((), (), s32[]{:S(2)}) async-start(), calls=%async_computation | async-start | bytes 7077888 | tf_op jit(solution)/shard_map/all_gather | solution.py:28
  34.3 133.0 %all-gather.13.cloned.1.call-start = ((), (), s32[]{:S(2)}) async-start(), calls=%async_computation.3 | async-start | bytes 1310720 | tf_op jit(solution)/shard_map/all_gather | solution.py:35
  35.1 171.6 %all-gather.11.cloned.1.call-start = ((), (), s32[]{:S(2)}) async-start(), calls=%async_computation.2 | async-start | bytes 10485760 | tf_op jit(solution)/shard_map/all_gather | solution.py:34
  35.7 0.7 copy-start.4
  35.7 230.7 %all-gather.17.cloned.1.call-start = ((), (), s32[]{:S(2)}) async-start(), calls=%async_computation.5 | async-start | bytes 10485760 | tf_op jit(solution)/shard_map/all_gather | solution.py:85
  36.3 295.3 %all-gather.15.cloned.1.call-start = ((), (), s32[]{:S(2)}) async-start(), calls=%async_computation.4 | async-start | bytes 3538944 | tf_op jit(solution)/shard_map/all_gather | solution.py:81
  220.5 118.9 %copy-start.3 = (f32[1024]{0:T(1024)S(1)}, f32[1024]{0:T(1024)}, u32[]{:S(2)}) copy-start(f32[1024]{0:T(1024)} %param.18) | copy-start | bytes 12292
  339.4 36.4 %copy-start.2 = (bf16[384,1024]{1,0:T(8,128)(2,1)}, bf16[384,1024]{1,0:T(8,128)(2,1)S(1)}, u32[]{:S(2)}) copy-start(bf16[384,1024]{1,0:T(8,128)(2,1)S(1)} %get-tuple-element.10) | copy-start | bytes 2359300
Sparse Core Ops, SparseCore 0:
  9.6 19.4 all-gather.8
  34.5 95.9 all-gather.6
  132.1 14.8 all-gather.12
  148.4 58.2 all-gather.10
  208.1 58.2 all-gather.16
  268.9 62.6 all-gather.14
where the time goes:
time: 383 us
  waiting for transfers between devices  208 us (54%)
  blocking collectives  120 us (31%)
  matrix products  32 us (8%)
  between operations  14.3 us (4%)
  other arithmetic  4.2 us (1%)
  local copies, waits for them, and re-layouts  4.01 us (1%)
    all_gather x1, waiting for transfers between devices, local(): lax.all_gather((xfloat * first_scale * attn_gain).astype(jnp.bfloat16), '...  93.9 us
    all_gather x1, waiting for transfers between devices, local(): mixed_all = lax.all_gather(attended, 'tp', axis=1, tiled=True)  65.2 us
    all_gather x1, waiting for transfers between devices, local(): lax.all_gather(output_weight, 'rep', axis=0, tiled=True)  45.9 us
    psum x1, blocking collectives, local(): total_out, weighted = lax.psum((squares, local_scores), 'tp')  34.3 us
    all_gather x1, blocking collectives, local(): lax.all_gather(key_rows, 'tp', axis=1, tiled=True)  31.1 us
    all_gather x1, blocking collectives, local(): lax.all_gather(value_rows, 'tp', axis=1, tiled=True)  31 us
    psum x1, blocking collectives, local(): total = lax.psum(jnp.sum(xfloat * xfloat, axis=1), 'tp')  23.1 us
    dot_general x3, matrix products, local(): jnp.dot(columns, piece, preferred_element_type=jnp.float32)  18.8 us
  transfers between devices with their start and end apart: 6, of which 4 were waited for; matrix products, arithmetic and copies ran while one was open for 8% of the time, Pallas kernels for 0%

commit v1 on v0

v1 whole, which is shorter than its diff:
```python
import functools
import jax
import jax.numpy as jnp
from jax import lax
from jax.experimental import pallas as pl
from jax.experimental.pallas import tpu as pltpu
from jax.sharding import PartitionSpec as P

KEY_VALUE_HEADS = 4
HEAD_SIZE = 128
EPS = 1e-05
MESH = pl.DeviceIdType.MESH


def slot(ref, dim, size, index):
    if dim is None:
        return ref.at[index]
    start = pl.multiple_of(index * size, size)
    return ref.at[pl.ds(start, size)] if dim == 0 else ref.at[:, pl.ds(start, size)]


class Line:
    def __init__(self, axis, count, dim, src, dst, sems):
        self.axis, self.dim, self.src, self.dst = axis, dim, src, dst
        self.count = count
        self.up_sem, self.down_sem, self.pair_sem, self.line_recv, self.pair_recv, self.own_sem = sems
        me = lax.axis_index(axis)
        self.me, self.place, self.side = me, me // 2, me % 2
        self.partner = me + 1 - 2 * self.side
        self.size = None if dim is None else src.shape[dim]

    def at(self, index):
        return slot(self.dst, self.dim, self.size, index)

    def copy(self, source, index, send, recv, target):
        return pltpu.make_async_remote_copy(
            src_ref=source,
            dst_ref=self.at(index),
            send_sem=send,
            recv_sem=recv,
            device_id={self.axis: target},
            device_id_type=MESH,
        )

    def up(self, source, origin):
        return self.copy(
            source, 2 * origin + self.side, self.up_sem.at[origin], self.line_recv.at[origin], self.me + 2
        )

    def down(self, source, origin):
        return self.copy(
            source, 2 * origin + self.side, self.down_sem.at[origin], self.line_recv.at[origin], self.me - 2
        )

    def pair(self, source, origin):
        return self.copy(
            source,
            2 * origin + self.side,
            self.pair_sem.at[origin],
            self.pair_recv.at[origin],
            self.partner,
        )

    def own(self):
        return pltpu.make_async_copy(self.src, self.at(self.me), self.own_sem.at[0])

    def has_up(self):
        return self.place < self.count - 1

    def has_down(self):
        return self.place > 0

    def begin(self):
        @pl.when(self.has_up())
        def _():
            self.up(self.src, self.place).start()

        @pl.when(self.has_down())
        def _():
            self.down(self.src, self.place).start()

        self.pair(self.src, self.place).start()
        self.own().start()

    def hop(self, step):
        below, above = self.place - step, self.place + step

        @pl.when(below >= 0)
        def _():
            block = self.at(2 * below + self.side)
            self.up(block, below).wait_recv()

            @pl.when(self.has_up())
            def _():
                self.up(block, below).start()

            self.pair(block, below).start()

        @pl.when(above < self.count)
        def _():
            block = self.at(2 * above + self.side)
            self.down(block, above).wait_recv()

            @pl.when(self.has_down())
            def _():
                self.down(block, above).start()

            self.pair(block, above).start()

    def finish(self):
        self.own().wait()
        for origin in range(self.count):
            here = self.at(2 * origin + self.side)
            self.pair(here, origin).wait_send()
            pltpu.make_async_remote_copy(
                src_ref=here,
                dst_ref=self.at(2 * origin + 1 - self.side),
                send_sem=self.pair_sem.at[origin],
                recv_sem=self.pair_recv.at[origin],
                device_id={self.axis: self.partner},
                device_id_type=MESH,
            ).wait_recv()

            @pl.when((origin <= self.place) & self.has_up())
            def _():
                self.up(here, origin).wait_send()

            @pl.when((origin >= self.place) & self.has_down())
            def _():
                self.down(here, origin).wait_send()

    def neighbours(self):
        return ((self.has_up(), self.me + 2), (self.has_down(), self.me - 2), (None, self.partner))


class Direct:
    def __init__(self, axis, members, src, dst, sems):
        self.axis, self.members, self.src, self.dst = axis, members, src, dst
        self.send, self.recv, self.own_sem = sems
        self.me = lax.axis_index(axis)

    def to(self, offset):
        return pltpu.make_async_remote_copy(
            src_ref=self.src,
            dst_ref=self.dst.at[self.me],
            send_sem=self.send.at[offset - 1],
            recv_sem=self.recv.at[offset - 1],
            device_id={self.axis: lax.rem(self.me + offset, self.members)},
            device_id_type=MESH,
        )

    def come(self, offset):
        return pltpu.make_async_remote_copy(
            src_ref=self.src,
            dst_ref=self.dst.at[lax.rem(self.me - offset + self.members, self.members)],
            send_sem=self.send.at[offset - 1],
            recv_sem=self.recv.at[offset - 1],
            device_id={self.axis: lax.rem(self.me + offset, self.members)},
            device_id_type=MESH,
        )

    def own(self):
        return pltpu.make_async_copy(self.src, self.dst.at[self.me], self.own_sem.at[0])

    def begin(self):
        for offset in range(1, self.members):
            self.to(offset).start()
        self.own().start()

    def finish(self):
        for offset in range(1, self.members):
            self.to(offset).wait_send()
            self.come(offset).wait_recv()
        self.own().wait()


def gather_kernel(plan, sizes, *refs):
    count = len(plan)
    sources, targets = refs[:count], refs[count : 2 * count]
    sems = list(refs[2 * count :])
    jobs = []
    for (kind, axis, dim), src, dst in zip(plan, sources, targets):
        if kind == "line":
            jobs.append(Line(axis, sizes[axis] // 2, dim, src, dst, sems[:6]))
            del sems[:6]
        else:
            jobs.append(Direct(axis, sizes[axis], src, dst, sems[:3]))
            del sems[:3]
    barrier = pltpu.get_barrier_semaphore()
    direct_axes = {job.axis for job in jobs if isinstance(job, Direct)}
    greeted, peers = set(), 0
    for job in jobs:
        if job.axis in greeted:
            continue
        greeted.add(job.axis)
        if job.axis in direct_axes:
            members = sizes[job.axis]
            peers = peers + members - 1
            for offset in range(1, members):
                pl.semaphore_signal(
                    barrier,
                    inc=1,
                    device_id={job.axis: lax.rem(job.me + offset, members)},
                    device_id_type=MESH,
                )
        else:
            for there, target in job.neighbours():
                def signal(target=target, job=job):
                    pl.semaphore_signal(
                        barrier, inc=1, device_id={job.axis: target}, device_id_type=MESH
                    )

                if there is None:
                    peers = peers + 1
                    signal()
                else:
                    peers = peers + there.astype(jnp.int32)
                    pl.when(there)(signal)
    pl.semaphore_wait(barrier, peers)
    for job in jobs:
        job.begin()
    lines = [job for job in jobs if isinstance(job, Line)]
    for step in range(1, max([job.count for job in lines], default=1)):
        for job in lines:
            if step < job.count:
                job.hop(step)
    for job in jobs:
        job.finish()


def gather(plan, sizes, arrays, collective_id, memory=pl.ANY):
    shapes, scratch = [], []
    for (kind, axis, dim), array in zip(plan, arrays):
        members = sizes[axis]
        if dim is None:
            shape = (members,) + array.shape
        else:
            shape = tuple(n * members if i == dim else n for i, n in enumerate(array.shape))
        shapes.append(jax.ShapeDtypeStruct(shape, array.dtype))
        if kind == "line":
            scratch += [pltpu.SemaphoreType.DMA((members // 2,))] * 5
        else:
            scratch += [pltpu.SemaphoreType.DMA((members - 1,))] * 2
        scratch += [pltpu.SemaphoreType.DMA((1,))]
    return pl.pallas_call(
        functools.partial(gather_kernel, plan, sizes),
        out_shape=tuple(shapes),
        in_specs=[pl.BlockSpec(memory_space=memory)] * len(arrays),
        out_specs=tuple([pl.BlockSpec(memory_space=memory)] * len(arrays)),
        scratch_shapes=scratch,
        compiler_params=pltpu.CompilerParams(collective_id=collective_id, has_side_effects=True),
    )(*arrays)


def local(
    sizes,
    tokens,
    row_lengths,
    attn_gain,
    query_weight,
    key_weight,
    value_matrix,
    output_weight,
    final_gain,
    value_head,
):
    width = tokens.shape[1] * sizes["tp"]
    rows_here = tokens.shape[0]
    head_cols = query_weight.shape[1]
    kv_cols = key_weight.shape[1]
    xfloat = tokens.astype(jnp.float32)
    squares_here = jnp.sum(xfloat * xfloat, axis=1)[None, :]
    gained = (xfloat * attn_gain).astype(jnp.bfloat16)
    packed = jnp.concatenate([query_weight, key_weight, value_matrix], axis=1)
    columns, weights, squares_all = gather(
        (("line", "tp", 1), ("line", "rep", 0), ("direct", "tp", None)),
        sizes,
        (gained, packed, squares_here),
        0,
    )
    first_scale = lax.rsqrt(jnp.sum(squares_all, axis=(0, 1)) / width + EPS)[:, None]
    projected = jnp.dot(columns, weights, preferred_element_type=jnp.float32)
    projected = (projected * first_scale).astype(jnp.bfloat16)
    query = projected[:, :head_cols]
    (kv_all,) = gather((("line", "tp", None),), sizes, (projected[:, head_cols:],), 1)
    sequence_rows = row_lengths.shape[0]
    length = rows_here // sequence_rows
    local_heads = head_cols // HEAD_SIZE
    key_full = kv_all[:, :, :kv_cols].transpose(1, 0, 2).reshape(rows_here, -1)
    value_full = kv_all[:, :, kv_cols:].transpose(1, 0, 2).reshape(rows_here, -1)
    first_head = lax.axis_index("tp") * local_heads
    key_value_index = (first_head + jnp.arange(local_heads, dtype=jnp.int32)) % KEY_VALUE_HEADS
    query4 = query.reshape(sequence_rows, length, local_heads, HEAD_SIZE)
    key4 = key_full.reshape(sequence_rows, length, KEY_VALUE_HEADS, HEAD_SIZE)
    value4 = value_full.reshape(sequence_rows, length, KEY_VALUE_HEADS, HEAD_SIZE)
    if local_heads % KEY_VALUE_HEADS or local_heads != KEY_VALUE_HEADS:
        key4 = jnp.take(key4, key_value_index, axis=2)
        value4 = jnp.take(value4, key_value_index, axis=2)
    scores = jnp.einsum(
        "rqhd,rkhd->rhqk", query4, key4, preferred_element_type=jnp.float32
    ) * (1.0 / HEAD_SIZE**0.5)
    position = jnp.arange(length, dtype=jnp.int32)
    causal = position[None, :] <= position[:, None]
    allowed = causal[None, None, :, :] & (
        position[None, None, None, :] < row_lengths[:, None, None, None]
    )
    scores = jnp.where(allowed, scores, jnp.float32(-1e30))
    scores = scores - jnp.max(scores, axis=3, keepdims=True)
    expo = jnp.exp(scores)
    probs = (expo / jnp.sum(expo, axis=3, keepdims=True)).astype(jnp.bfloat16)
    attended = jnp.einsum(
        "rhqk,rkhd->rqhd", probs, value4, preferred_element_type=jnp.float32
    )
    attended = attended.astype(jnp.bfloat16).reshape(rows_here, head_cols)
    mixed, out_weights = gather(
        (("line", "tp", 1), ("line", "rep", 0)), sizes, (attended, output_weight), 2
    )
    update = jnp.dot(mixed, out_weights, preferred_element_type=jnp.float32)
    resid_out = (xfloat + update).astype(jnp.bfloat16)
    rfloat = resid_out.astype(jnp.float32)
    squares = jnp.sum(rfloat * rfloat, axis=1)
    local_scores = jnp.dot(rfloat * final_gain, value_head, precision=lax.Precision.HIGHEST)
    stats = jnp.concatenate([local_scores.T, squares[None, :]], axis=0)
    (stats_all,) = gather((("direct", "tp", None),), sizes, (stats,), 3)
    stats = jnp.sum(stats_all, axis=0)
    logits = (stats[:-1] * lax.rsqrt(stats[-1:] / width + EPS)).T
    live = (position[None, :] < row_lengths[:, None]).reshape(rows_here, 1)
    objective_scores = jnp.where(live, logits, jnp.float32(0.0))
    return (resid_out, objective_scores)


def solution(mesh):
    in_specs = (
        P("rep", "tp"),
        P("rep"),
        P("tp"),
        P("rep", "tp"),
        P("rep", "tp"),
        P("rep", "tp"),
        P("rep", "tp"),
        P("tp"),
        P("tp", None),
    )
    out_specs = (P("rep", "tp"), P("rep", None))
    body = functools.partial(local, dict(mesh.shape))
    return jax.shard_map(body, mesh=mesh, in_specs=in_specs, out_specs=out_specs, check_vma=False)
```

time: 383 us -> 249 us (0.65)
  Pallas kernels: 0 us -> 212 us
  waiting for transfers between devices: 208 us -> 0 us
  blocking collectives: 120 us -> 0 us
  between operations: 14.3 us -> 0.87 us
  matrix products: 32 us -> 20.8 us
    pallas_call x0 -> x4, Pallas kernels: none -> 212 us  [gather(): pl.pallas_call(functools.partial(gather_kernel, plan, sizes), out_shape=t...]
    all_gather x6 -> x0, waiting for transfers between devices: 206 us -> none  [the longest x1 93.9 us: local(): lax.all_gather((xfloat * first_scale * attn_gain).astype(jnp.bfloat16), '...]
    all_gather x2 -> x0, blocking collectives: 62.1 us -> none  [the longest x1 31.1 us: local(): lax.all_gather(key_rows, 'tp', axis=1, tiled=True)]
    psum x2 -> x0, blocking collectives: 57.4 us -> none  [the longest x1 34.3 us: local(): total_out, weighted = lax.psum((squares, local_scores), 'tp')]
    dot_general x5 -> x3, matrix products: 28.7 us -> 18.6 us  [the longest x1 10.2 us: local(): projected = jnp.dot(columns, weights, preferred_element_type=jnp.float32)]
  transfers between devices with their start and end apart: 6 -> 0, of which waited for: 4 -> 0; matrix products, arithmetic and copies ran while one was open for 8% -> 0% of each run, Pallas kernels for 0% -> 0%
where the time goes in v1:
time: 249 us
  Pallas kernels  212 us (85%)
  matrix products  20.8 us (8%)
  other arithmetic  7.4 us (3%)
  local copies, waits for them, and re-layouts  6.93 us (3%)
    pallas_call x4, Pallas kernels, gather(): pl.pallas_call(functools.partial(gather_kernel, plan, sizes), out_shape=t...  212 us
    dot_general x1, matrix products, local(): projected = jnp.dot(columns, weights, preferred_element_type=jnp.float32)  10.2 us
    dot_general x1, matrix products, local(): update = jnp.dot(mixed, out_weights, preferred_element_type=jnp.float32)  7.88 us

profile of v1, /device:TPU:0, one launch (start us, length us, event | category | flops | bytes accessed | tf_op | source)
XLA Modules:
  0.0 248.5 jit_solution(4469634647524218725)
XLA Ops:
  0.6 0.0 copy-start
  0.7 2.4 fusion.5
  3.1 0.6 broadcast_in_dim.24.refs_2_
  3.6 1.2 copy.16
  4.9 0.3 copy.17
  5.2 1.9 pad_maximum_fusion.refs_1_
  7.0 110.8 %shard_map.104 = (bf16[384,8192]{1,0:T(8,128)(2,1)}, bf16[8192,640]{1,0:T(8,128)(2,1)}, f32[8,1,384]{2,1,0:T(1,128)}) custom-call(bf16[384,1024]{1,0:T(8,128)(2,1)} %get-tuple-element.15.refs_0_, bf16[2048,640]{1,0:T(8,128)(2,1)} %pad_maximum_fusion.refs_1_, f32[1,384]{1,0:T(1,128)} %broadcast_in_dim.24.refs_2_), custom_call_target="tpu_custom_call" | custom-call | tf_op jit(solution)/shard_map/pallas_call | solution.py:245
  117.9 0.7 reduce_sum.46
  118.6 10.2 %fusion.8 = bf16[384,640]{1,0:T(8,128)(2,1)S(1)} fusion(bf16[384,8192]{1,0:T(8,128)(2,1)} %get-tuple-element.7, bf16[8192,640]{1,0:T(8,128)(2,1)} %get-tuple-element.8, f32[384]{0:T(512)S(1)} %add_rsqrt_fusion), kind=kOutput, calls=%fused_computation.17 | convolution fusion | flops 4027023360 | bytes 17270272 | tf_op jit(solution)/shard_map/dot_general | solution.py:282
  128.9 0.6 slice.24.refs_0_
  129.5 16.4 %shard_map.105 = bf16[8,384,128]{2,1,0:T(8,128)(2,1)} custom-call(bf16[384,128]{1,0:T(8,128)(2,1)} %slice.24.refs_0_), custom_call_target="tpu_custom_call" | custom-call | tf_op jit(solution)/shard_map/pallas_call | solution.py:245
  145.9 1.7 slice_bitcast_fusion.1
  147.6 0.0 copy-start.6
  147.6 0.3 copy.19
  148.0 0.3 reshape_reshape.7
  148.3 0.1 reshape.74
  148.4 0.1 iota_compare_fusion.1
  148.5 0.1 broadcast_and_fusion
  148.6 0.8 fusion.31
  149.4 0.3 copy.18
  149.7 0.3 reshape_reshape.6
  150.0 0.5 fusion.9
  150.5 0.3 copy.24
  150.8 0.8 copy.46
  151.6 78.3 %shard_map.106 = (bf16[384,4096]{1,0:T(8,128)(2,1)}, bf16[4096,1024]{1,0:T(8,128)(2,1)}) custom-call(bf16[384,512]{1,0:T(8,128)(2,1)} %bitcast.24, bf16[1024,1024]{1,0:T(8,128)(2,1)} %refs_1_.1), custom_call_target="tpu_custom_call" | custom-call | tf_op jit(solution)/shard_map/pallas_call | solution.py:245
  230.0 7.9 %fusion.3 = (f32[384]{0:T(512)S(1)}, bf16[384,1024]{1,0:T(8,128)(2,1)S(1)}) fusion(bf16[384,4096]{1,0:T(8,128)(2,1)} %get-tuple-element.10, bf16[4096,1024]{1,0:T(8,128)(2,1)} %get-tuple-element.11, bf16[384,1024]{1,0:T(8,128)(2,1)S(1)} %copy-done.2), kind=kOutput, calls=%fused_computation.9 | convolution fusion | flops 3223584256 | bytes 13108736 | tf_op jit(solution)/shard_map/dot_general | solution.py:318
  237.9 1.5 fusion.10
  239.4 0.6 pad_maximum_fusion.1.refs_0_
  240.0 6.9 %shard_map.107 = f32[8,7,384]{2,1,0:T(8,128)} custom-call(f32[7,384]{1,0:T(8,128)} %pad_maximum_fusion.1.refs_0_), custom_call_target="tpu_custom_call" | custom-call | tf_op jit(solution)/shard_map/pallas_call | solution.py:245
  246.9 0.9 reduce_sum.49
  247.8 0.1 lt.35
  247.9 0.6 fusion.20
  (17 shorter events, 0.1 us)
Async XLA Ops:
  0.6 237.2 %copy-start = (f32[1024,6]{0,1:T(8,128)S(1)}, f32[1024,6]{0,1:T(8,128)}, u32[]{:S(2)}) copy-start(f32[1024,6]{0,1:T(8,128)} %param.17) | copy-start | bytes 73732
  0.6 4.2 %copy-start.4 = (bf16[2048,64]{0,1:T(8,128)(2,1)S(1)}, bf16[2048,64]{0,1:T(8,128)(2,1)}, u32[]{:S(2)}) copy-start(bf16[2048,64]{0,1:T(8,128)(2,1)} %param.14) | copy-start | bytes 786436
  0.7 4.5 %copy-start.1 = (bf16[2048,512]{1,0:T(8,128)(2,1)S(1)}, bf16[2048,512]{1,0:T(8,128)(2,1)}, u32[]{:S(2)}) copy-start(bf16[2048,512]{1,0:T(8,128)(2,1)} %param.12) | copy-start | bytes 6291460
  147.6 0.8 copy-start.6
  150.5 79.5 %copy-start.2 = (bf16[384,1024]{1,0:T(8,128)(2,1)S(1)}, bf16[384,1024]{1,0:T(8,128)(2,1)}, u32[]{:S(2)}) copy-start(bf16[384,1024]{1,0:T(8,128)(2,1)} %param.9) | copy-start | bytes 2359300
  230.0 7.9 %copy-start.5 = (f32[1024]{0:T(1024)S(1)}, f32[1024]{0:T(1024)}, u32[]{:S(2)}) copy-start(f32[1024]{0:T(1024)} %param.16) | copy-start | bytes 12292
  237.9 10.7 %copy-start.3 = (bf16[384,1024]{1,0:T(8,128)(2,1)}, bf16[384,1024]{1,0:T(8,128)(2,1)S(1)}, u32[]{:S(2)}) copy-start(bf16[384,1024]{1,0:T(8,128)(2,1)S(1)} %get-tuple-element.19) | copy-start | bytes 2359300

commit v2 on v1

--- a/solution.py
+++ b/solution.py
@@ -12,25 +12,39 @@
 MESH = pl.DeviceIdType.MESH
 
 
-def slot(ref, dim, size, index):
+class Stage:
+    def __init__(self, src, dst, buffer, sems):
+        self.into = pltpu.make_async_copy(src, buffer, sems.at[0])
+        self.out = pltpu.make_async_copy(buffer, dst, sems.at[1])
+
+
+def slot(ref, dim, size, index, rows=None):
+    if rows is not None:
+        return ref.at[pl.ds(*rows), pl.ds(pl.multiple_of(index * size, size), size)]
     if dim is None:
         return ref.at[index]
+    if isinstance(dim, tuple):
+        return ref.at[index, pl.ds(dim[2], dim[1])]
     start = pl.multiple_of(index * size, size)
     return ref.at[pl.ds(start, size)] if dim == 0 else ref.at[:, pl.ds(start, size)]
 
 
 class Line:
-    def __init__(self, axis, count, dim, src, dst, sems):
-        self.axis, self.dim, self.src, self.dst = axis, dim, src, dst
+    def __init__(self, axis, count, dim, src, dst, sems, rows=None):
+        self.axis, self.dim, self.dst = axis, dim, dst
+        self.windowed = isinstance(dim, tuple)
+        rows = dim[:2] if self.windowed else rows
+        self.src = src if rows is None else src.at[pl.ds(*rows)]
+        self.rows = None if self.windowed else rows
         self.count = count
-        self.up_sem, self.down_sem, self.pair_sem, self.line_recv, self.pair_recv, self.own_sem = sems
+        self.up_sem, self.down_sem, self.pair_sem, self.line_recv, self.pair_recv = sems
         me = lax.axis_index(axis)
         self.me, self.place, self.side = me, me // 2, me % 2
         self.partner = me + 1 - 2 * self.side
-        self.size = None if dim is None else src.shape[dim]
+        self.size = None if dim is None or self.windowed else src.shape[dim]
 
     def at(self, index):
-        return slot(self.dst, self.dim, self.size, index)
+        return slot(self.dst, self.dim, self.size, index, self.rows)
 
     def copy(self, source, index, send, recv, target):
         return pltpu.make_async_remote_copy(
@@ -61,8 +75,8 @@
             self.partner,
         )
 
-    def own(self):
-        return pltpu.make_async_copy(self.src, self.at(self.me), self.own_sem.at[0])
+    def own_block(self):
+        return self.at(self.me)
 
     def has_up(self):
         return self.place < self.count - 1
@@ -80,7 +94,6 @@
             self.down(self.src, self.place).start()
 
         self.pair(self.src, self.place).start()
-        self.own().start()
 
     def hop(self, step):
         below, above = self.place - step, self.place + step
@@ -108,7 +121,6 @@
             self.pair(block, above).start()
 
     def finish(self):
-        self.own().wait()
         for origin in range(self.count):
             here = self.at(2 * origin + self.side)
             self.pair(here, origin).wait_send()
@@ -133,10 +145,75 @@
         return ((self.has_up(), self.me + 2), (self.has_down(), self.me - 2), (None, self.partner))
 
 
+class Cross(Line):
+    def __init__(self, axis, count, dim, src, dst, sems, rows):
+        super().__init__(axis, count, dim, src, dst, sems, rows)
+        self.other = 1 - self.side
+
+    def along(self, source, origin, side, which, step):
+        sem = self.up_sem if step > 0 else self.down_sem
+        return self.copy(
+            source,
+            2 * origin + side,
+            sem.at[which * self.count + origin],
+            self.line_recv.at[which * self.count + origin],
+            self.me + step,
+        )
+
+    def spread(self, source, origin, which):
+        side = self.side if which == 0 else self.other
+
+        @pl.when(self.has_up() & (origin <= self.place))
+        def _():
+            self.along(source, origin, side, which, 2).start()
+
+        @pl.when(self.has_down() & (origin >= self.place))
+        def _():
+            self.along(source, origin, side, which, -2).start()
+
+    def across(self, index, source):
+        return self.copy(source, index, self.pair_sem.at[0], self.pair_recv.at[0], self.partner)
+
+    def begin(self):
+        self.across(self.me, self.src).start()
+        self.spread(self.src, self.place, 0)
+
+    def turn(self):
+        theirs = self.at(self.partner)
+        self.across(self.partner, theirs).wait_recv()
+        self.spread(theirs, self.place, 1)
+
+    def hop(self, step):
+        for which in range(2):
+            side = self.side if which == 0 else self.other
+            for origin in (self.place - step, self.place + step):
+
+                @pl.when((origin >= 0) & (origin < self.count))
+                def _(origin=origin, side=side, which=which):
+                    block = self.at(2 * origin + side)
+                    self.along(block, origin, side, which, 2).wait_recv()
+                    self.spread(block, origin, which)
+
+    def finish(self):
+        self.across(self.me, self.src).wait_send()
+        for which in range(2):
+            side = self.side if which == 0 else self.other
+            for origin in range(self.count):
+                block = self.at(2 * origin + side)
+
+                @pl.when((origin <= self.place) & self.has_up())
+                def _(origin=origin, side=side, which=which, block=block):
+                    self.along(block, origin, side, which, 2).wait_send()
+
+                @pl.when((origin >= self.place) & self.has_down())
+                def _(origin=origin, side=side, which=which, block=block):
+                    self.along(block, origin, side, which, -2).wait_send()
+
+
 class Direct:
     def __init__(self, axis, members, src, dst, sems):
         self.axis, self.members, self.src, self.dst = axis, members, src, dst
-        self.send, self.recv, self.own_sem = sems
+        self.send, self.recv = sems
         self.me = lax.axis_index(axis)
 
     def to(self, offset):
@@ -159,33 +236,50 @@
             device_id_type=MESH,
         )
 
-    def own(self):
-        return pltpu.make_async_copy(self.src, self.dst.at[self.me], self.own_sem.at[0])
+    def own_block(self):
+        return self.dst.at[self.me]
 
     def begin(self):
         for offset in range(1, self.members):
             self.to(offset).start()
-        self.own().start()
 
     def finish(self):
         for offset in range(1, self.members):
             self.to(offset).wait_send()
             self.come(offset).wait_recv()
-        self.own().wait()
 
 
 def gather_kernel(plan, sizes, *refs):
     count = len(plan)
     sources, targets = refs[:count], refs[count : 2 * count]
-    sems = list(refs[2 * count :])
-    jobs = []
+    rest = list(refs[2 * count :])
+
+    def take(number):
+        taken = rest[:number]
+        del rest[:number]
+        return taken
+
+    jobs, stages = [], []
     for (kind, axis, dim), src, dst in zip(plan, sources, targets):
-        if kind == "line":
-            jobs.append(Line(axis, sizes[axis] // 2, dim, src, dst, sems[:6]))
-            del sems[:6]
+        if kind == "fill":
+            dst = targets[dim]
+            buffer, sems = take(2)
+            stages.append(Stage(src, dst.at[:, pl.ds(0, src.shape[1])], buffer, sems))
+            continue
+        if kind == "direct":
+            made = [Direct(axis, sizes[axis], src, dst, take(2))]
+        elif kind == "line":
+            made = [Line(axis, sizes[axis] // 2, dim, src, dst, take(5))]
         else:
-            jobs.append(Direct(axis, sizes[axis], src, dst, sems[:3]))
-            del sems[:3]
+            first, second = cut(src.shape[0])
+            made = [
+                Line(axis, sizes[axis] // 2, dim, src, dst, take(5), first),
+                Cross(axis, sizes[axis] // 2, dim, src, dst, take(5), second),
+            ]
+        for job in made:
+            buffer, sems = take(2)
+            stages.append(Stage(job.src, job.own_block(), buffer, sems))
+        jobs += made
     barrier = pltpu.get_barrier_semaphore()
     direct_axes = {job.axis for job in jobs if isinstance(job, Direct)}
     greeted, peers = set(), 0
@@ -219,29 +313,57 @@
     pl.semaphore_wait(barrier, peers)
     for job in jobs:
         job.begin()
-    lines = [job for job in jobs if isinstance(job, Line)]
-    for step in range(1, max([job.count for job in lines], default=1)):
-        for job in lines:
-            if step < job.count:
+    for stage in stages:
+        stage.into.start()
+    for stage in stages:
+        stage.into.wait()
+        stage.out.start()
+    for job in jobs:
+        if isinstance(job, Cross):
+            job.turn()
+    for axis in ("tp", "rep"):
+        lines = [job for job in jobs if isinstance(job, Line) and job.axis == axis]
+        for step in range(1, max([job.count for job in lines], default=1)):
+            for job in lines:
                 job.hop(step)
     for job in jobs:
         job.finish()
+    for stage in stages:
+        stage.out.wait()
+
+
+def cut(total):
+    cross = total // (6 * 16) * 16
+    return (0, total - cross), (total - cross, cross)
 
 
 def gather(plan, sizes, arrays, collective_id, memory=pl.ANY):
     shapes, scratch = [], []
+    dma = pltpu.SemaphoreType.DMA
     for (kind, axis, dim), array in zip(plan, arrays):
+        if kind == "fill":
+            shapes.append(jax.ShapeDtypeStruct((8, 128), array.dtype))
+            scratch += [pltpu.VMEM(array.shape, array.dtype), dma((2,))]
+            continue
         members = sizes[axis]
         if dim is None:
             shape = (members,) + array.shape
+        elif isinstance(dim, tuple):
+            shape = (members, dim[2] + dim[1]) + array.shape[1:]
         else:
             shape = tuple(n * members if i == dim else n for i, n in enumerate(array.shape))
         shapes.append(jax.ShapeDtypeStruct(shape, array.dtype))
-        if kind == "line":
-            scratch += [pltpu.SemaphoreType.DMA((members // 2,))] * 5
+        whole = pltpu.VMEM(array.shape, array.dtype)
+        if kind == "direct":
+            scratch += [dma((members - 1,))] * 2 + [whole, dma((2,))]
+        elif kind == "line":
+            if isinstance(dim, tuple):
+                whole = pltpu.VMEM(dim[1:2] + array.shape[1:], array.dtype)
+            scratch += [dma((members // 2,))] * 5 + [whole, dma((2,))]
         else:
-            scratch += [pltpu.SemaphoreType.DMA((members - 1,))] * 2
-        scratch += [pltpu.SemaphoreType.DMA((1,))]
+            scratch += [dma((members // 2,))] * 5 + [dma((members,))] * 5
+            for _, length in cut(array.shape[0]):
+                scratch += [pltpu.VMEM((length,) + array.shape[1:], array.dtype), dma((2,))]
     return pl.pallas_call(
         functools.partial(gather_kernel, plan, sizes),
         out_shape=tuple(shapes),
@@ -272,8 +394,13 @@
     squares_here = jnp.sum(xfloat * xfloat, axis=1)[None, :]
     gained = (xfloat * attn_gain).astype(jnp.bfloat16)
     packed = jnp.concatenate([query_weight, key_weight, value_matrix], axis=1)
+    early = output_weight.shape[0] // 4
     columns, weights, squares_all = gather(
-        (("line", "tp", 1), ("line", "rep", 0), ("direct", "tp", None)),
+        (
+            ("split", "tp", 1),
+            ("line", "rep", 0),
+            ("direct", "tp", None),
+        ),
         sizes,
         (gained, packed, squares_here),
         0,
@@ -282,7 +409,12 @@
     projected = jnp.dot(columns, weights, preferred_element_type=jnp.float32)
     projected = (projected * first_scale).astype(jnp.bfloat16)
     query = projected[:, :head_cols]
-    (kv_all,) = gather((("line", "tp", None),), sizes, (projected[:, head_cols:],), 1)
+    kv_all, out_early = gather(
+        (("line", "tp", None), ("line", "rep", (0, early, 0))),
+        sizes,
+        (projected[:, head_cols:], output_weight),
+        1,
+    )
     sequence_rows = row_lengths.shape[0]
     length = rows_here // sequence_rows
     local_heads = head_cols // HEAD_SIZE
@@ -312,9 +444,14 @@
         "rhqk,rkhd->rqhd", probs, value4, preferred_element_type=jnp.float32
     )
     attended = attended.astype(jnp.bfloat16).reshape(rows_here, head_cols)
-    mixed, out_weights = gather(
-        (("line", "tp", 1), ("line", "rep", 0)), sizes, (attended, output_weight), 2
-    )
+    late = (early, output_weight.shape[0] - early, early)
+    mixed, out_weights, _ = gather(
+        (("split", "tp", 1), ("line", "rep", late), ("fill", "rep", 1)),
+        sizes,
+        (attended, output_weight, out_early),
+        2,
+    )
+    out_weights = out_weights.reshape(-1, tokens.shape[1])
     update = jnp.dot(mixed, out_weights, preferred_element_type=jnp.float32)
     resid_out = (xfloat + update).astype(jnp.bfloat16)
     rfloat = resid_out.astype(jnp.float32)

time: 249 us -> 178 us (0.71)
  Pallas kernels: 212 us -> 142 us
    pallas_call x4, Pallas kernels: 212 us -> 142 us  [gather(): pl.pallas_call(functools.partial(gather_kernel, plan, sizes), out_shape=t...]
where the time goes in v2:
time: 178 us
  Pallas kernels  142 us (80%)
  matrix products  20.8 us (12%)
  other arithmetic  7.4 us (4%)
  local copies, waits for them, and re-layouts  6.93 us (4%)
    pallas_call x4, Pallas kernels, gather(): pl.pallas_call(functools.partial(gather_kernel, plan, sizes), out_shape=t...  142 us
    dot_general x1, matrix products, local(): projected = jnp.dot(columns, weights, preferred_element_type=jnp.float32)  10.2 us
    dot_general x1, matrix products, local(): update = jnp.dot(mixed, out_weights, preferred_element_type=jnp.float32)  7.88 us

profile of v2, /device:TPU:0, one launch (start us, length us, event | category | flops | bytes accessed | tf_op | source)
XLA Modules:
  0.0 178.1 jit_solution(16996969420648595291)
XLA Ops:
  0.6 0.0 copy-start
  0.7 2.4 %fusion.5 = (f32[384]{0:T(512)S(1)}, bf16[384,1024]{1,0:T(8,128)(2,1)}) fusion(bf16[384,1024]{1,0:T(8,128)(2,1)} %param.9, f32[1024]{0:T(1024)} %param.11), kind=kLoop, calls=%fused_computation.11 | loop fusion | flops 1965696 | bytes 1578496 | tf_op jit(solution)/shard_map/reduce_sum | solution.py:394
  3.1 0.6 broadcast_in_dim.24.refs_2_
  3.6 1.2 copy.16
  4.9 0.3 copy.17
  5.2 1.9 %pad_maximum_fusion.refs_1_ = bf16[2048,640]{1,0:T(8,128)(2,1)} fusion(bf16[2048,64]{1,0:T(8,128)(2,1)S(1)} %copy.17, bf16[2048,64]{1,0:T(8,128)(2,1)S(1)} %copy.16, bf16[2048,512]{1,0:T(8,128)(2,1)S(1)} %copy-done.1), kind=kLoop, calls=%fused_computation.1 | loop fusion | flops 7864320 | bytes 5242880 | tf_op jit(solution)/shard_map/concatenate | solution.py:396
  7.0 77.4 %shard_map.104 = (bf16[384,8192]{1,0:T(8,128)(2,1)}, bf16[8192,640]{1,0:T(8,128)(2,1)}, f32[8,1,384]{2,1,0:T(1,128)}) custom-call(bf16[384,1024]{1,0:T(8,128)(2,1)} %get-tuple-element.19.refs_0_, bf16[2048,640]{1,0:T(8,128)(2,1)} %pad_maximum_fusion.refs_1_, f32[1,384]{1,0:T(1,128)} %broadcast_in_dim.24.refs_2_), custom_call_target="tpu_custom_call" | custom-call | tf_op jit(solution)/shard_map/pallas_call | solution.py:367
  84.4 0.7 reduce_sum.46
  85.2 10.2 %fusion.8 = bf16[384,640]{1,0:T(8,128)(2,1)S(1)} fusion(bf16[384,8192]{1,0:T(8,128)(2,1)} %get-tuple-element.9, bf16[8192,640]{1,0:T(8,128)(2,1)} %get-tuple-element.10, f32[384]{0:T(512)S(1)} %add_rsqrt_fusion), kind=kOutput, calls=%fused_computation.17 | convolution fusion | flops 4027023360 | bytes 17270272 | tf_op jit(solution)/shard_map/dot_general | solution.py:409
  95.4 0.6 slice.24.refs_0_
  96.0 16.8 %shard_map.105 = (bf16[8,384,128]{2,1,0:T(8,128)(2,1)}, bf16[4,256,1024]{2,1,0:T(8,128)(2,1)}) custom-call(bf16[384,128]{1,0:T(8,128)(2,1)} %slice.24.refs_0_, bf16[1024,1024]{1,0:T(8,128)(2,1)} %refs_1_.3), custom_call_target="tpu_custom_call" | custom-call | tf_op jit(solution)/shard_map/pallas_call | solution.py:367
  112.8 1.7 slice_bitcast_fusion.1
  114.5 0.0 copy-start.6
  114.5 0.3 copy.19
  114.8 0.3 reshape_reshape.7
  115.2 0.1 reshape.77
  115.3 0.1 iota_compare_fusion.1
  115.4 0.1 broadcast_and_fusion
  115.5 0.8 fusion.31
  116.3 0.3 copy.18
  116.6 0.3 reshape_reshape.6
  116.9 0.5 fusion.9
  117.4 0.3 copy.24
  117.7 0.8 copy.46
  118.5 40.9 %shard_map.106 = (bf16[384,4096]{1,0:T(8,128)(2,1)}, bf16[4,1024,1024]{2,1,0:T(8,128)(2,1)}, bf16[8,128]{1,0:T(8,128)(2,1)}) custom-call(bf16[384,512]{1,0:T(8,128)(2,1)} %bitcast.25, bf16[1024,1024]{1,0:T(8,128)(2,1)} %refs_1_.3, bf16[4,256,1024]{2,1,0:T(8,128)(2,1)} %get-tuple-element.13.refs_2_), custom_call_target="tpu_custom_call" | custom-call | tf_op jit(solution)/shard_map/pallas_call | solution.py:367
  159.4 7.9 %fusion.3 = (f32[384]{0:T(512)S(1)}, bf16[384,1024]{1,0:T(8,128)(2,1)S(1)}) fusion(bf16[384,4096]{1,0:T(8,128)(2,1)} %get-tuple-element.14, bf16[4096,1024]{1,0:T(8,128)(2,1)} %bitcast.27, bf16[384,1024]{1,0:T(8,128)(2,1)S(1)} %copy-done.2), kind=kOutput, calls=%fused_computation.9 | convolution fusion | flops 3223584256 | bytes 13108736 | tf_op jit(solution)/shard_map/dot_general | solution.py:455
  167.3 1.5 fusion.10
  168.8 0.6 pad_maximum_fusion.1.refs_0_
  169.4 7.0 %shard_map.107 = f32[8,7,384]{2,1,0:T(8,128)} custom-call(f32[7,384]{1,0:T(8,128)} %pad_maximum_fusion.1.refs_0_), custom_call_target="tpu_custom_call" | custom-call | tf_op jit(solution)/shard_map/pallas_call | solution.py:367
  176.4 0.9 reduce_sum.49
  177.4 0.1 lt.35
  177.4 0.6 fusion.20
  (17 shorter events, 0.1 us)
Async XLA Ops:
  0.6 166.7 %copy-start = (f32[1024,6]{0,1:T(8,128)S(1)}, f32[1024,6]{0,1:T(8,128)}, u32[]{:S(2)}) copy-start(f32[1024,6]{0,1:T(8,128)} %param.17) | copy-start | bytes 73732
  0.6 4.2 %copy-start.4 = (bf16[2048,64]{0,1:T(8,128)(2,1)S(1)}, bf16[2048,64]{0,1:T(8,128)(2,1)}, u32[]{:S(2)}) copy-start(bf16[2048,64]{0,1:T(8,128)(2,1)} %param.14) | copy-start | bytes 786436
  0.7 4.5 %copy-start.1 = (bf16[2048,512]{1,0:T(8,128)(2,1)S(1)}, bf16[2048,512]{1,0:T(8,128)(2,1)}, u32[]{:S(2)}) copy-start(bf16[2048,512]{1,0:T(8,128)(2,1)} %param.12) | copy-start | bytes 6291460
  114.5 0.8 copy-start.6
  118.5 40.9 %copy-start.2 = (bf16[384,1024]{1,0:T(8,128)(2,1)S(1)}, bf16[384,1024]{1,0:T(8,128)(2,1)}, u32[]{:S(2)}) copy-start(bf16[384,1024]{1,0:T(8,128)(2,1)} %param.9) | copy-start | bytes 2359300
  159.4 7.9 %copy-start.5 = (f32[1024]{0:T(1024)S(1)}, f32[1024]{0:T(1024)}, u32[]{:S(2)}) copy-start(f32[1024]{0:T(1024)} %param.16) | copy-start | bytes 12292
  167.3 10.8 %copy-start.3 = (bf16[384,1024]{1,0:T(8,128)(2,1)}, bf16[384,1024]{1,0:T(8,128)(2,1)S(1)}, u32[]{:S(2)}) copy-start(bf16[384,1024]{1,0:T(8,128)(2,1)S(1)} %get-tuple-element.23) | copy-start | bytes 2359300

commit v3 on v2

--- a/solution.py
+++ b/solution.py
@@ -264,7 +264,7 @@
         if kind == "fill":
             dst = targets[dim]
             buffer, sems = take(2)
-            stages.append(Stage(src, dst.at[:, pl.ds(0, src.shape[1])], buffer, sems))
+            stages.append(Stage(src, dst.at[:, pl.ds(axis, src.shape[1])], buffer, sems))
             continue
         if kind == "direct":
             made = [Direct(axis, sizes[axis], src, dst, take(2))]
@@ -394,15 +394,17 @@
     squares_here = jnp.sum(xfloat * xfloat, axis=1)[None, :]
     gained = (xfloat * attn_gain).astype(jnp.bfloat16)
     packed = jnp.concatenate([query_weight, key_weight, value_matrix], axis=1)
+    first = output_weight.shape[0] // 16
     early = output_weight.shape[0] // 4
-    columns, weights, squares_all = gather(
+    columns, weights, out_first, squares_all = gather(
         (
             ("split", "tp", 1),
             ("line", "rep", 0),
+            ("line", "rep", (0, first, 0)),
             ("direct", "tp", None),
         ),
         sizes,
-        (gained, packed, squares_here),
+        (gained, packed, output_weight, squares_here),
         0,
     )
     first_scale = lax.rsqrt(jnp.sum(squares_all, axis=(0, 1)) / width + EPS)[:, None]
@@ -410,7 +412,7 @@
     projected = (projected * first_scale).astype(jnp.bfloat16)
     query = projected[:, :head_cols]
     kv_all, out_early = gather(
-        (("line", "tp", None), ("line", "rep", (0, early, 0))),
+        (("line", "tp", None), ("line", "rep", (first, early, 0))),
         sizes,
         (projected[:, head_cols:], output_weight),
         1,
@@ -444,11 +446,12 @@
         "rhqk,rkhd->rqhd", probs, value4, preferred_element_type=jnp.float32
     )
     attended = attended.astype(jnp.bfloat16).reshape(rows_here, head_cols)
-    late = (early, output_weight.shape[0] - early, early)
-    mixed, out_weights, _ = gather(
-        (("split", "tp", 1), ("line", "rep", late), ("fill", "rep", 1)),
+    before = first + early
+    late = (before, output_weight.shape[0] - before, before)
+    mixed, out_weights, _, _ = gather(
+        (("split", "tp", 1), ("line", "rep", late), ("fill", 0, 1), ("fill", first, 1)),
         sizes,
-        (attended, output_weight, out_early),
+        (attended, output_weight, out_first, out_early),
         2,
     )
     out_weights = out_weights.reshape(-1, tokens.shape[1])

time: 178 us -> 178 us (level)
  no operation moved by 1% of the time
where the time goes in v3:
time: 178 us; the launch traced here: 177 us
  Pallas kernels  141 us (79%)
  matrix products  20.8 us (12%)
  other arithmetic  7.4 us (4%)
  local copies, waits for them, and re-layouts  6.93 us (4%)
    pallas_call x4, Pallas kernels, gather(): pl.pallas_call(functools.partial(gather_kernel, plan, sizes), out_shape=t...  141 us
    dot_general x1, matrix products, local(): projected = jnp.dot(columns, weights, preferred_element_type=jnp.float32)  10.2 us
    dot_general x1, matrix products, local(): update = jnp.dot(mixed, out_weights, preferred_element_type=jnp.float32)  7.88 us

profile of v3, /device:TPU:0, one launch (start us, length us, event | category | flops | bytes accessed | tf_op | source)
XLA Modules:
  0.0 177.2 jit_solution(16792197451573032325)
XLA Ops:
  0.6 0.0 copy-start
  0.7 2.4 %fusion.5 = (f32[384]{0:T(512)S(1)}, bf16[384,1024]{1,0:T(8,128)(2,1)}) fusion(bf16[384,1024]{1,0:T(8,128)(2,1)} %param.9, f32[1024]{0:T(1024)} %param.11), kind=kLoop, calls=%fused_computation.11 | loop fusion | flops 1965696 | bytes 1578496 | tf_op jit(solution)/shard_map/reduce_sum | solution.py:394
  3.1 0.6 broadcast_in_dim.24.refs_3_
  3.6 1.2 copy.16
  4.9 0.3 copy.17
  5.2 1.9 %pad_maximum_fusion.refs_1_ = bf16[2048,640]{1,0:T(8,128)(2,1)} fusion(bf16[2048,64]{1,0:T(8,128)(2,1)S(1)} %copy.17, bf16[2048,64]{1,0:T(8,128)(2,1)S(1)} %copy.16, bf16[2048,512]{1,0:T(8,128)(2,1)S(1)} %copy-done.1), kind=kLoop, calls=%fused_computation.1 | loop fusion | flops 7864320 | bytes 5242880 | tf_op jit(solution)/shard_map/concatenate | solution.py:396
  7.0 77.5 %shard_map.104 = (bf16[384,8192]{1,0:T(8,128)(2,1)}, bf16[8192,640]{1,0:T(8,128)(2,1)}, bf16[4,64,1024]{2,1,0:T(8,128)(2,1)}, f32[8,1,384]{2,1,0:T(1,128)}) custom-call(bf16[384,1024]{1,0:T(8,128)(2,1)} %get-tuple-element.21.refs_0_, bf16[2048,640]{1,0:T(8,128)(2,1)} %pad_maximum_fusion.refs_1_, bf16[1024,1024]{1,0:T(8,128)(2,1)} %refs_1_.3, ...), custom_call_target="tpu_custom_call" | custom-call | tf_op jit(solution)/shard_map/pallas_call | solution.py:367
  84.5 0.7 reduce_sum.46
  85.3 10.2 %fusion.8 = bf16[384,640]{1,0:T(8,128)(2,1)S(1)} fusion(bf16[384,8192]{1,0:T(8,128)(2,1)} %get-tuple-element.10, bf16[8192,640]{1,0:T(8,128)(2,1)} %get-tuple-element.11, f32[384]{0:T(512)S(1)} %add_rsqrt_fusion), kind=kOutput, calls=%fused_computation.17 | convolution fusion | flops 4027023360 | bytes 17270272 | tf_op jit(solution)/shard_map/dot_general | solution.py:411
  95.5 0.6 slice.24.refs_0_
  96.1 16.8 %shard_map.105 = (bf16[8,384,128]{2,1,0:T(8,128)(2,1)}, bf16[4,256,1024]{2,1,0:T(8,128)(2,1)}) custom-call(bf16[384,128]{1,0:T(8,128)(2,1)} %slice.24.refs_0_, bf16[1024,1024]{1,0:T(8,128)(2,1)} %refs_1_.3), custom_call_target="tpu_custom_call" | custom-call | tf_op jit(solution)/shard_map/pallas_call | solution.py:367
  112.9 1.7 slice_bitcast_fusion.1
  114.6 0.0 copy-start.6
  114.6 0.3 copy.19
  114.9 0.3 reshape_reshape.7
  115.3 0.1 reshape.77
  115.4 0.1 iota_compare_fusion.1
  115.5 0.1 broadcast_and_fusion
  115.6 0.8 fusion.31
  116.4 0.3 copy.18
  116.7 0.3 reshape_reshape.6
  117.0 0.5 fusion.9
  117.5 0.3 copy.24
  117.8 0.8 copy.46
  118.6 40.1 %shard_map.106 = (bf16[384,4096]{1,0:T(8,128)(2,1)}, bf16[4,1024,1024]{2,1,0:T(8,128)(2,1)}, bf16[8,128]{1,0:T(8,128)(2,1)}, bf16[8,128]{1,0:T(8,128)(2,1)}) custom-call(bf16[384,512]{1,0:T(8,128)(2,1)} %bitcast.25, bf16[1024,1024]{1,0:T(8,128)(2,1)} %refs_1_.3, bf16[4,64,1024]{2,1,0:T(8,128)(2,1)} %get-tuple-element.14.refs_2_, ...), custom_call_target="tpu_custom_call" | custom-call | tf_op jit(solution)/shard_map/pallas_call | solution.py:367
  158.7 7.9 %fusion.3 = (f32[384]{0:T(512)S(1)}, bf16[384,1024]{1,0:T(8,128)(2,1)S(1)}) fusion(bf16[384,4096]{1,0:T(8,128)(2,1)} %get-tuple-element.16, bf16[4096,1024]{1,0:T(8,128)(2,1)} %bitcast.27, bf16[384,1024]{1,0:T(8,128)(2,1)S(1)} %copy-done.2), kind=kOutput, calls=%fused_computation.9 | convolution fusion | flops 3223584256 | bytes 13108736 | tf_op jit(solution)/shard_map/dot_general | solution.py:458
  166.6 1.5 fusion.10
  168.1 0.6 pad_maximum_fusion.1.refs_0_
  168.7 6.9 %shard_map.107 = f32[8,7,384]{2,1,0:T(8,128)} custom-call(f32[7,384]{1,0:T(8,128)} %pad_maximum_fusion.1.refs_0_), custom_call_target="tpu_custom_call" | custom-call | tf_op jit(solution)/shard_map/pallas_call | solution.py:367
  175.6 0.9 reduce_sum.49
  176.5 0.1 lt.35
  176.6 0.6 fusion.20
  (17 shorter events, 0.1 us)
Async XLA Ops:
  0.6 166.0 %copy-start = (f32[1024,6]{0,1:T(8,128)S(1)}, f32[1024,6]{0,1:T(8,128)}, u32[]{:S(2)}) copy-start(f32[1024,6]{0,1:T(8,128)} %param.17) | copy-start | bytes 73732
  0.6 4.2 %copy-start.4 = (bf16[2048,64]{0,1:T(8,128)(2,1)S(1)}, bf16[2048,64]{0,1:T(8,128)(2,1)}, u32[]{:S(2)}) copy-start(bf16[2048,64]{0,1:T(8,128)(2,1)} %param.14) | copy-start | bytes 786436
  0.7 4.5 %copy-start.1 = (bf16[2048,512]{1,0:T(8,128)(2,1)S(1)}, bf16[2048,512]{1,0:T(8,128)(2,1)}, u32[]{:S(2)}) copy-start(bf16[2048,512]{1,0:T(8,128)(2,1)} %param.12) | copy-start | bytes 6291460
  114.6 0.8 copy-start.6
  118.6 40.1 %copy-start.2 = (bf16[384,1024]{1,0:T(8,128)(2,1)S(1)}, bf16[384,1024]{1,0:T(8,128)(2,1)}, u32[]{:S(2)}) copy-start(bf16[384,1024]{1,0:T(8,128)(2,1)} %param.9) | copy-start | bytes 2359300
  158.7 7.9 %copy-start.5 = (f32[1024]{0:T(1024)S(1)}, f32[1024]{0:T(1024)}, u32[]{:S(2)}) copy-start(f32[1024]{0:T(1024)} %param.16) | copy-start | bytes 12292
  166.6 10.6 %copy-start.3 = (bf16[384,1024]{1,0:T(8,128)(2,1)}, bf16[384,1024]{1,0:T(8,128)(2,1)S(1)}, u32[]{:S(2)}) copy-start(bf16[384,1024]{1,0:T(8,128)(2,1)S(1)} %get-tuple-element.25) | copy-start | bytes 2359300
